TPU v7x, 32 devices: a whole 2x2x4 slice. The times are simulated.
32 devices in a mesh: blk: 8 (over z, x), rows: 4 (over y, core).
Axes of the slice: x: 2, y: 2, z: 4, core: 2. Of those that a mesh axis runs over, the one named last changes fastest.
Arguments:
- columns: float32 [512, 16384], P('blk', 'rows'), may hold values from -100 to 100
- plan: int32 [3, 16], replicated, may hold values from 0 to 15, as said below
Outputs:
- swept: float32 [512, 16384], P('blk', 'rows')
- off_ratio: float32 [3], replicated
Inputs may be any that keep to these rules, and one draw needn't show every extreme that they name: `plan`: row s is a permutation of the 16 positions (position k is slot k % 2 of blk index k // 2). In each row there are a slot t and a number m of 1 to 7 such that the block in slot t of every blk index i goes to slot t of blk index (i + m) modulo 16 / 2, and every other block stays where it is.
All inputs are finite; a program needn't handle non-finite values. Where the computation divides by a largest or mean magnitude, that divisor is 1e-20 or more.
Results may differ from a plain program's by a relative error of at most 0.00011.
Values sent between devices are 32-bit elements; how exact they have to be, the bound alone decides.
No kernel may reach another device: no remote copies, remote signals or barrier semaphores. Data moves between devices by JAX's collectives and lax.ppermute only.
A program may use at most 64 MiB of HBM per device.

v0:
```python
from functools import partial
import jax
import jax.numpy as jnp
from jax import lax
from jax.sharding import PartitionSpec as P

STEPS = 3
EIG_ITERS = 3
NS_ITERS = 8
PRECISE = lax.Precision.HIGHEST


def shifted(value, axis, steps):
    count = lax.axis_size(axis)
    pairs = [(source, (source + steps) % count) for source in range(count)]
    return lax.ppermute(value, axis, pairs)


def matmul(left, right):
    return jnp.matmul(left, right, precision=PRECISE, preferred_element_type=jnp.float32)


def orthonormal(matrix):
    lengths = jnp.sqrt(jnp.sum(matrix * matrix, axis=0, keepdims=True))
    normed = matrix / lengths
    inner = matmul(normed.T, normed)
    bound = jnp.max(jnp.sum(jnp.abs(inner), axis=1))
    normed = normed / jnp.sqrt(bound)
    for turn_index in range(NS_ITERS):
        normed = 1.5 * normed - 0.5 * matmul(normed, matmul(normed.T, normed))
    return normed


def pair_rotation(gram_sum):
    rotation = jnp.eye(gram_sum.shape[0], dtype=gram_sum.dtype)
    for turn_index in range(EIG_ITERS):
        rotation = orthonormal(matmul(gram_sum, rotation))
    return rotation


def move_by(values, distance):
    return shifted(values, "blk", distance)


def local(columns, plan):
    block_width = columns.shape[0] // 2
    cycle_size = lax.axis_size("blk")
    eye_mask = jnp.eye(2 * block_width, dtype=bool)
    current = columns
    off_list = []
    diag_list = []
    for step_index in range(STEPS):
        partial_gram = matmul(current, current.T)
        gram_sum = lax.psum(partial_gram, "rows")
        off_part = jnp.where(eye_mask, 0.0, gram_sum)
        diag_part = jnp.where(eye_mask, gram_sum, 0.0)
        off_local = jnp.sum(off_part * off_part)
        diag_local = jnp.sum(diag_part * diag_part)
        off_total, diag_total = lax.psum((off_local, diag_local), "blk")
        off_list.append(off_total)
        diag_list.append(diag_total)
        rotation = pair_rotation(gram_sum)
        rotated = matmul(rotation.T, current)
        first_dest = plan[step_index, 0]
        second_dest = plan[step_index, 1]
        partner_step = jnp.maximum(first_dest // 2, second_dest // 2)
        leaving_high = second_dest != 1
        moving = jnp.where(leaving_high, rotated[block_width:], rotated[:block_width])
        staying = jnp.where(leaving_high, rotated[:block_width], rotated[block_width:])
        branches = [partial(move_by, distance=distance) for distance in range(1, cycle_size)]
        moving = lax.switch(partner_step - 1, branches, moving)
        current = jnp.where(
            leaving_high,
            jnp.concatenate([staying, moving], axis=0),
            jnp.concatenate([moving, staying], axis=0),
        )
    off_sums = jnp.stack(off_list)
    diag_sums = jnp.stack(diag_list)
    return (current, jnp.sqrt(off_sums) / jnp.sqrt(diag_sums))


def solution(mesh):
    return jax.shard_map(
        local,
        mesh=mesh,
        in_specs=(P("blk", "rows"), P()),
        out_specs=(P("blk", "rows"), P()),
        check_vma=False,
    )
```

profile of v0, /device:TPU:0, one launch (start us, length us, event | category | flops | bytes accessed | tf_op | source)
XLA Modules:
  0.0 189.1 jit_solution(8808458993383925959)
XLA Ops:
  0.6 1.6 fusion.124
  19.2 1.0 fusion.125
  20.2 12.9 %psum.63 = f32[64,64]{1,0:T(8,128)S(1)} all-reduce(f32[64,64]{1,0:T(8,128)S(1)} %fusion.125), channel_id=1, replica_groups=mesh['blk'=8,'rows'=4] {'rows'}, use_global_device_ids=true, to_apply=%region_0.0 | all-reduce | flops 4096 | bytes 32768 | tf_op jit(solution)/shard_map/psum | solution.py:54
  33.1 0.7 multiply_reduce_fusion.2
  49.1 1.0 fusion.147
  50.2 13.9 %conditional.3 = (f32[32,4096]{1,0:T(8,128)}) conditional(s32[]{:T(128)} %clamp.9, f32[32,4096]{1,0:T(8,128)S(1)} %get-tuple-element.64, f32[32,4096]{1,0:T(8,128)S(1)} %get-tuple-element.64, f32[32,4096]{1,0:T(8,128)S(1)} %get-tuple-element.64, f32[32,4096]{1,0:T(8,128)S(1)} %get-tuple-element.64, ...), branch_computations={%region_10.11_spmd, %region_11.12_spmd, %region_12.13_spmd, %regio... | conditional | bytes 2097200 | solution.py:71
  50.2 3.7 %collective-permute-start.5 = (f32[32,4096]{1,0:T(8,128)S(1)}, f32[32,4096]{1,0:T(8,128)}, u32[]{:S(2)}, u32[]{:S(2)}) collective-permute-start(f32[32,4096]{1,0:T(8,128)S(1)} %param.5), channel_id=1, source_target_pairs={{0,24},{4,28},{8,0},{12,4},{16,8},{20,12},{24,16},{28,20},{1,25},{... | collective-permute-start | bytes 1572872 | tf_op jit(solution)/shard_map/cond/branch_5_fun/ppermute | solution.py:16
  53.9 10.2 %collective-permute-done.5 = f32[32,4096]{1,0:T(8,128)} collective-permute-done((f32[32,4096]{1,0:T(8,128)S(1)}, f32[32,4096]{1,0:T(8,128)}, u32[]{:S(2)}, u32[]{:S(2)}) %collective-permute-start.5) | collective-permute-done | bytes 524320 | tf_op jit(solution)/shard_map/cond/branch_5_fun/ppermute | solution.py:16
  64.0 2.7 %fusion.84 = f32[64,64]{1,0:T(8,128)S(1)} fusion(f32[32,4096]{1,0:T(8,128)} %get-tuple-element.89, f32[32,4096]{1,0:T(8,128)S(1)} %get-tuple-element.63, pred[]{:T(512)S(6)} %ne.49), kind=kOutput, calls=%fused_computation.168 | convolution fusion | flops 202113024 | bytes 1064961 | tf_op jit(solution)/shard_map/dot_general | solution.py:20
  66.8 10.7 %psum.64 = f32[64,64]{1,0:T(8,128)S(1)} all-reduce(f32[64,64]{1,0:T(8,128)S(1)} %fusion.84), channel_id=1, replica_groups=mesh['blk'=8,'rows'=4] {'rows'}, use_global_device_ids=true, to_apply=%region_17.18 | all-reduce | flops 4096 | bytes 32768 | tf_op jit(solution)/shard_map/psum | solution.py:54
  77.5 0.7 multiply_reduce_fusion.1
  93.4 2.3 %fusion.83 = f32[64,4096]{1,0:T(8,128)S(1)} fusion(f32[64,64]{1,0:T(8,128)S(1)} %fusion.24, f32[32,4096]{1,0:T(8,128)} %get-tuple-element.89, f32[32,4096]{1,0:T(8,128)S(1)} %get-tuple-element.63, pred[]{:T(512)S(6)} %ne.49), kind=kOutput, calls=%fused_computation.167 | convolution fusion | flops 202113024 | bytes 2113537 | tf_op jit(solution)/shard_map/dot_general | solution.py:20
  95.8 27.1 %conditional.4 = (f32[32,4096]{1,0:T(8,128)}) conditional(s32[]{:T(128)} %clamp.10, f32[32,4096]{1,0:T(8,128)S(1)} %get-tuple-element.62, f32[32,4096]{1,0:T(8,128)S(1)} %get-tuple-element.62, f32[32,4096]{1,0:T(8,128)S(1)} %get-tuple-element.62, f32[32,4096]{1,0:T(8,128)S(1)} %get-tuple-element.62, ...), branch_computations={%region_27.28_spmd, %region_28.29_spmd, %region_29.30_spmd, %regio... | conditional | bytes 2097200 | solution.py:71
  95.8 1.5 collective-permute-start.9
  97.4 25.6 %collective-permute-done.9 = f32[32,4096]{1,0:T(8,128)} collective-permute-done((f32[32,4096]{1,0:T(8,128)S(1)}, f32[32,4096]{1,0:T(8,128)}, u32[]{:S(2)}, u32[]{:S(2)}) %collective-permute-start.9) | collective-permute-done | bytes 524320 | tf_op jit(solution)/shard_map/cond/branch_2_fun/ppermute | solution.py:16
  122.9 2.7 %fusion.82 = f32[64,64]{1,0:T(8,128)S(1)} fusion(f32[32,4096]{1,0:T(8,128)} %get-tuple-element.90, f32[32,4096]{1,0:T(8,128)S(1)} %get-tuple-element.61, pred[]{:T(512)S(6)} %ne.48), kind=kOutput, calls=%fused_computation.166 | convolution fusion | flops 202113024 | bytes 1064961 | tf_op jit(solution)/shard_map/dot_general | solution.py:20
  125.7 10.3 %psum.65 = f32[64,64]{1,0:T(8,128)S(1)} all-reduce(f32[64,64]{1,0:T(8,128)S(1)} %fusion.82), channel_id=1, replica_groups=mesh['blk'=8,'rows'=4] {'rows'}, use_global_device_ids=true, to_apply=%region_34.35 | all-reduce | flops 4096 | bytes 32768 | tf_op jit(solution)/shard_map/psum | solution.py:54
  136.6 18.0 %all-reduce = (f32[1]{0:T(128)}, f32[1]{0:T(128)}, f32[1]{0:T(128)}, f32[1]{0:T(128)}, f32[1]{0:T(128)}, /*index=5*/f32[1]{0:T(128)}) all-reduce(f32[1]{0:T(128)} %bitcast.8, f32[1]{0:T(128)} %bitcast.7, f32[1]{0:T(128)} %bitcast.6, f32[1]{0:T(128)} %bitcast.11, f32[1]{0:T(128)} %bitcast.10, ...), channel_id=1, replica_groups=mesh['blk'=8,'rows'=4] {'blk'}, use_global_device_ids=true, to_apply=%region_56.57 | all-reduce | flops 6 | bytes 48 | tf_op jit(solution)/shard_map/psum | solution.py:59
  154.6 4.3 %fusion.119 = f32[3]{0:T(128)} fusion(f32[1]{0:T(128)} %get-tuple-element.53, f32[1]{0:T(128)} %get-tuple-element.54, f32[1]{0:T(128)} %get-tuple-element.55, f32[1]{0:T(128)} %get-tuple-element.56, f32[1]{0:T(128)} %get-tuple-element.57, f32[1]{0:T(128)} %get-tuple-element.58), kind=kLoop, calls=%fused_computation.235 | loop fusion | flops 15 | bytes 36 | tf_op jit(solution)/shard_map/div | solution.py:79
  174.2 2.3 %fusion.81 = f32[64,4096]{1,0:T(8,128)S(1)} fusion(f32[64,64]{1,0:T(8,128)S(1)} %fusion, f32[32,4096]{1,0:T(8,128)} %get-tuple-element.90, f32[32,4096]{1,0:T(8,128)S(1)} %get-tuple-element.61, pred[]{:T(512)S(6)} %ne.48), kind=kOutput, calls=%fused_computation.165 | convolution fusion | flops 202113024 | bytes 2113537 | tf_op jit(solution)/shard_map/dot_general | solution.py:20
  176.6 10.3 %conditional.5 = (f32[32,4096]{1,0:T(8,128)}) conditional(s32[]{:T(128)} %clamp.11, f32[32,4096]{1,0:T(8,128)S(1)} %get-tuple-element.60, f32[32,4096]{1,0:T(8,128)S(1)} %get-tuple-element.60, f32[32,4096]{1,0:T(8,128)S(1)} %get-tuple-element.60, f32[32,4096]{1,0:T(8,128)S(1)} %get-tuple-element.60, ...), branch_computations={%region_44.45_spmd, %region_45.46_spmd, %region_46.47_spmd, %regio... | conditional | bytes 2097200 | solution.py:71
  176.6 2.1 %collective-permute-start.20 = (f32[32,4096]{1,0:T(8,128)S(1)}, f32[32,4096]{1,0:T(8,128)}, u32[]{:S(2)}, u32[]{:S(2)}) collective-permute-start(f32[32,4096]{1,0:T(8,128)S(1)} %param.20), channel_id=1, source_target_pairs={{0,28},{4,0},{8,4},{12,8},{16,12},{20,16},{24,20},{28,24},{1,29},{... | collective-permute-start | bytes 1572872 | tf_op jit(solution)/shard_map/cond/branch_6_fun/ppermute | solution.py:16
  178.7 8.2 %collective-permute-done.20 = f32[32,4096]{1,0:T(8,128)} collective-permute-done((f32[32,4096]{1,0:T(8,128)S(1)}, f32[32,4096]{1,0:T(8,128)}, u32[]{:S(2)}, u32[]{:S(2)}) %collective-permute-start.20) | collective-permute-done | bytes 524320 | tf_op jit(solution)/shard_map/cond/branch_6_fun/ppermute | solution.py:16
  186.8 2.3 %maximum_select_fusion.2 = f32[64,4096]{1,0:T(8,128)} fusion(f32[32,4096]{1,0:T(8,128)} %get-tuple-element.91, f32[32,4096]{1,0:T(8,128)S(1)} %get-tuple-element.59, pred[]{:T(512)S(6)} %ne.47), kind=kLoop, calls=%fused_computation.164 | loop fusion | flops 786432 | bytes 2097153 | tf_op jit(solution)/shard_map/jit(_where)/select_n | solution.py:72
  (195 shorter events, 39.1 us)
Async XLA Ops:
  0.6 18.6 %copy-start = (f32[64,4096]{1,0:T(8,128)S(1)}, f32[64,4096]{1,0:T(8,128)}, u32[]{:S(2)}) copy-start(f32[64,4096]{1,0:T(8,128)} %param.23) | copy-start | bytes 3145732
  50.2 13.8 %collective-permute-start.5 = (f32[32,4096]{1,0:T(8,128)S(1)}, f32[32,4096]{1,0:T(8,128)}, u32[]{:S(2)}, u32[]{:S(2)}) collective-permute-start(f32[32,4096]{1,0:T(8,128)S(1)} %param.5), channel_id=1, source_target_pairs={{0,24},{4,28},{8,0},{12,4},{16,8},{20,12},{24,16},{28,20},{1,25},{... | collective-permute-start | bytes 1572872 | tf_op jit(solution)/shard_map/cond/branch_5_fun/ppermute | solution.py:16
  95.8 27.1 %collective-permute-start.9 = (f32[32,4096]{1,0:T(8,128)S(1)}, f32[32,4096]{1,0:T(8,128)}, u32[]{:S(2)}, u32[]{:S(2)}) collective-permute-start(f32[32,4096]{1,0:T(8,128)S(1)} %param.9), channel_id=1, source_target_pairs={{0,12},{4,16},{8,20},{12,24},{16,28},{20,0},{24,4},{28,8},{1,13},{... | collective-permute-start | bytes 1572872 | tf_op jit(solution)/shard_map/cond/branch_2_fun/ppermute | solution.py:16
  176.6 10.2 %collective-permute-start.20 = (f32[32,4096]{1,0:T(8,128)S(1)}, f32[32,4096]{1,0:T(8,128)}, u32[]{:S(2)}, u32[]{:S(2)}) collective-permute-start(f32[32,4096]{1,0:T(8,128)S(1)} %param.20), channel_id=1, source_target_pairs={{0,28},{4,0},{8,4},{12,8},{16,12},{20,16},{24,20},{28,24},{1,29},{... | collective-permute-start | bytes 1572872 | tf_op jit(solution)/shard_map/cond/branch_6_fun/ppermute | solution.py:16
where the time goes:
time: 190 us; the launch traced here: 189 us
  blocking collectives  51.9 us (27%)
  matrix products  44.7 us (24%)
  waiting for transfers between devices  43.9 us (23%)
  between operations  25.2 us (13%)
  other arithmetic  14.3 us (8%)
  starting transfers between devices  7.26 us (4%)
    dot_general x168, matrix products, matmul(): jnp.matmul(left, right, precision=PRECISE, preferred_element_type=jnp.flo...  44.7 us
    ppermute x3, waiting for transfers between devices, shifted(): return lax.ppermute(value, axis, pairs)  43.9 us
    psum x3, blocking collectives, local(): gram_sum = lax.psum(partial_gram, 'rows')  33.9 us
    psum x1, blocking collectives, local(): off_total, diag_total = lax.psum((off_local, diag_local), 'blk')  18 us
    ppermute x3, starting transfers between devices, shifted(): return lax.ppermute(value, axis, pairs)  7.26 us
    reduce_max x9, other arithmetic, orthonormal(): bound = jnp.max(jnp.sum(jnp.abs(inner), axis=1))  5.47 us
    div x1, other arithmetic, local(): return (current, jnp.sqrt(off_sums) / jnp.sqrt(diag_sums))  4.33 us
  transfers between devices with their start and end apart: 3, of which 3 were waited for; matrix products, arithmetic and copies ran while one was open for 0% of the time, Pallas kernels for 0%

commit v1 on v0

--- a/solution.py
+++ b/solution.py
@@ -51,7 +51,11 @@
     diag_list = []
     for step_index in range(STEPS):
         partial_gram = matmul(current, current.T)
-        gram_sum = lax.psum(partial_gram, "rows")
+        gram_sum = partial_gram
+        for hop in (1, 2):
+            gram_sum = gram_sum + lax.ppermute(
+                gram_sum, "rows", [(dev, dev ^ hop) for dev in range(4)]
+            )
         off_part = jnp.where(eye_mask, 0.0, gram_sum)
         diag_part = jnp.where(eye_mask, gram_sum, 0.0)
         off_local = jnp.sum(off_part * off_part)

time: 190 us -> 172 us (0.905)
  blocking collectives: 51.9 us -> 20.8 us
  waiting for transfers between devices: 43.9 us -> 53.6 us
  starting transfers between devices: 7.26 us -> 10.9 us
    psum x3 -> x0, blocking collectives: 33.9 us -> none  [local(): gram_sum = lax.psum(partial_gram, 'rows')]
    ppermute x3, waiting for transfers between devices: 43.9 us -> 50.3 us  [shifted(): return lax.ppermute(value, axis, pairs)]
    ppermute x0 -> x6, starting transfers between devices: none -> 5.64 us  [local(): lax.ppermute(gram_sum, 'rows', [(dev, dev ^ hop) for dev in range(4)])]
    ppermute x0 -> x6, waiting for transfers between devices: none -> 3.26 us  [local(): lax.ppermute(gram_sum, 'rows', [(dev, dev ^ hop) for dev in range(4)])]
    psum x1, blocking collectives: 18 us -> 20.8 us  [local(): off_total, diag_total = lax.psum((off_local, diag_local), 'blk')]
    ppermute x3, starting transfers between devices: 7.26 us -> 5.26 us  [shifted(): return lax.ppermute(value, axis, pairs)]
  transfers between devices with their start and end apart: 3 -> 9, of which waited for: 3 -> 6; matrix products, arithmetic and copies ran while one was open for 0% -> 0% of each run, Pallas kernels for 0% -> 0%
where the time goes in v1:
time: 172 us
  waiting for transfers between devices  53.6 us (31%)
  matrix products  44.7 us (26%)
  between operations  25.3 us (15%)
  blocking collectives  20.8 us (12%)
  other arithmetic  14.4 us (8%)
  starting transfers between devices  10.9 us (6%)
  local copies, waits for them, and re-layouts  1.95 us (1%)
    ppermute x3, waiting for transfers between devices, shifted(): return lax.ppermute(value, axis, pairs)  50.3 us
    dot_general x168, matrix products, matmul(): jnp.matmul(left, right, precision=PRECISE, preferred_element_type=jnp.flo...  44.7 us
    psum x1, blocking collectives, local(): off_total, diag_total = lax.psum((off_local, diag_local), 'blk')  20.8 us
    ppermute x6, starting transfers between devices, local(): lax.ppermute(gram_sum, 'rows', [(dev, dev ^ hop) for dev in range(4)])  5.64 us
    reduce_max x9, other arithmetic, orthonormal(): bound = jnp.max(jnp.sum(jnp.abs(inner), axis=1))  5.47 us
    ppermute x3, starting transfers between devices, shifted(): return lax.ppermute(value, axis, pairs)  5.26 us
    div x1, other arithmetic, local(): return (current, jnp.sqrt(off_sums) / jnp.sqrt(diag_sums))  4.33 us
  transfers between devices with their start and end apart: 9, of which 6 were waited for; matrix products, arithmetic and copies ran while one was open for 0% of the time, Pallas kernels for 0%

profile of v1, /device:TPU:0, one launch (start us, length us, event | category | flops | bytes accessed | tf_op | source)
XLA Modules:
  0.0 171.7 jit_solution(522474329371897323)
XLA Ops:
  0.6 1.2 copy-done
  1.9 1.0 fusion.116
  3.4 0.9 collective-permute-done.21
  4.3 2.9 %collective-permute-start.22 = (f32[64,64]{1,0:T(8,128)S(1)}, f32[64,64]{1,0:T(8,128)S(1)}, u32[]{:S(2)}, u32[]{:S(2)}) collective-permute-start(f32[64,64]{1,0:T(8,128)S(1)} %add.39), channel_id=1, source_target_pairs={{0,2},{1,3},{2,0},{3,1},{4,6},{5,7},{6,4},{7,5},{8,10},{9,11},{10,... | collective-permute-start | bytes 49160 | tf_op jit(solution)/shard_map/ppermute | solution.py:56
  29.7 1.0 fusion.138
  30.8 14.9 %conditional.3 = (f32[32,4096]{1,0:T(8,128)}) conditional(s32[]{:T(128)} %clamp.9, f32[32,4096]{1,0:T(8,128)S(1)} %get-tuple-element.67, f32[32,4096]{1,0:T(8,128)S(1)} %get-tuple-element.67, f32[32,4096]{1,0:T(8,128)S(1)} %get-tuple-element.67, f32[32,4096]{1,0:T(8,128)S(1)} %get-tuple-element.67, ...), branch_computations={%region_9.10_spmd, %region_10.11_spmd, %region_11.12_spmd, %region... | conditional | bytes 2097200 | solution.py:75
  30.8 3.7 %collective-permute-start.5 = (f32[32,4096]{1,0:T(8,128)S(1)}, f32[32,4096]{1,0:T(8,128)}, u32[]{:S(2)}, u32[]{:S(2)}) collective-permute-start(f32[32,4096]{1,0:T(8,128)S(1)} %param.5), channel_id=1, source_target_pairs={{0,24},{4,28},{8,0},{12,4},{16,8},{20,12},{24,16},{28,20},{1,25},{... | collective-permute-start | bytes 1572872 | tf_op jit(solution)/shard_map/cond/branch_5_fun/ppermute | solution.py:16
  34.5 11.2 %collective-permute-done.5 = f32[32,4096]{1,0:T(8,128)} collective-permute-done((f32[32,4096]{1,0:T(8,128)S(1)}, f32[32,4096]{1,0:T(8,128)}, u32[]{:S(2)}, u32[]{:S(2)}) %collective-permute-start.5) | collective-permute-done | bytes 524320 | tf_op jit(solution)/shard_map/cond/branch_5_fun/ppermute | solution.py:16
  45.7 2.7 %fusion.75 = f32[64,64]{1,0:T(8,128)S(1)} fusion(f32[32,4096]{1,0:T(8,128)} %get-tuple-element.92, f32[32,4096]{1,0:T(8,128)S(1)} %get-tuple-element.66, pred[]{:T(512)S(6)} %ne.49), kind=kOutput, calls=%fused_computation.159 | convolution fusion | flops 202113024 | bytes 1064961 | tf_op jit(solution)/shard_map/dot_general | solution.py:20
  48.5 1.2 collective-permute-done.23
  49.7 0.9 collective-permute-start.24
  72.2 2.3 %fusion.74 = f32[64,4096]{1,0:T(8,128)S(1)} fusion(f32[64,64]{1,0:T(8,128)S(1)} %fusion.21, f32[32,4096]{1,0:T(8,128)} %get-tuple-element.92, f32[32,4096]{1,0:T(8,128)S(1)} %get-tuple-element.66, pred[]{:T(512)S(6)} %ne.49), kind=kOutput, calls=%fused_computation.158 | convolution fusion | flops 202113024 | bytes 2113537 | tf_op jit(solution)/shard_map/dot_general | solution.py:20
  74.5 26.9 %conditional.4 = (f32[32,4096]{1,0:T(8,128)}) conditional(s32[]{:T(128)} %clamp.10, f32[32,4096]{1,0:T(8,128)S(1)} %get-tuple-element.65, f32[32,4096]{1,0:T(8,128)S(1)} %get-tuple-element.65, f32[32,4096]{1,0:T(8,128)S(1)} %get-tuple-element.65, f32[32,4096]{1,0:T(8,128)S(1)} %get-tuple-element.65, ...), branch_computations={%region_25.26_spmd, %region_26.27_spmd, %region_27.28_spmd, %regio... | conditional | bytes 2097200 | solution.py:75
  74.6 1.5 collective-permute-start.9
  76.1 25.4 %collective-permute-done.9 = f32[32,4096]{1,0:T(8,128)} collective-permute-done((f32[32,4096]{1,0:T(8,128)S(1)}, f32[32,4096]{1,0:T(8,128)}, u32[]{:S(2)}, u32[]{:S(2)}) %collective-permute-start.9) | collective-permute-done | bytes 524320 | tf_op jit(solution)/shard_map/cond/branch_2_fun/ppermute | solution.py:16
  101.5 2.7 %fusion.73 = f32[64,64]{1,0:T(8,128)S(1)} fusion(f32[32,4096]{1,0:T(8,128)} %get-tuple-element.93, f32[32,4096]{1,0:T(8,128)S(1)} %get-tuple-element.64, pred[]{:T(512)S(6)} %ne.48), kind=kOutput, calls=%fused_computation.157 | convolution fusion | flops 202113024 | bytes 1064961 | tf_op jit(solution)/shard_map/dot_general | solution.py:20
  104.3 1.2 collective-permute-done.25
  105.5 1.1 collective-permute-start.26
  128.0 2.3 %fusion.72 = f32[64,4096]{1,0:T(8,128)S(1)} fusion(f32[64,64]{1,0:T(8,128)S(1)} %fusion, f32[32,4096]{1,0:T(8,128)} %get-tuple-element.93, f32[32,4096]{1,0:T(8,128)S(1)} %get-tuple-element.64, pred[]{:T(512)S(6)} %ne.48), kind=kOutput, calls=%fused_computation.156 | convolution fusion | flops 202113024 | bytes 2113537 | tf_op jit(solution)/shard_map/dot_general | solution.py:20
  130.4 13.9 %conditional.5 = (f32[32,4096]{1,0:T(8,128)}) conditional(s32[]{:T(128)} %clamp.11, f32[32,4096]{1,0:T(8,128)S(1)} %get-tuple-element.63, f32[32,4096]{1,0:T(8,128)S(1)} %get-tuple-element.63, f32[32,4096]{1,0:T(8,128)S(1)} %get-tuple-element.63, f32[32,4096]{1,0:T(8,128)S(1)} %get-tuple-element.63, ...), branch_computations={%region_41.42_spmd, %region_42.43_spmd, %region_43.44_spmd, %regio... | conditional | bytes 2097200 | solution.py:75
  130.5 13.8 %collective-permute-done.20 = f32[32,4096]{1,0:T(8,128)} collective-permute-done((f32[32,4096]{1,0:T(8,128)S(1)}, f32[32,4096]{1,0:T(8,128)}, u32[]{:S(2)}, u32[]{:S(2)}) %collective-permute-start.20) | collective-permute-done | bytes 524320 | tf_op jit(solution)/shard_map/cond/branch_6_fun/ppermute | solution.py:16
  144.3 2.3 %maximum_select_fusion.2 = f32[64,4096]{1,0:T(8,128)} fusion(f32[32,4096]{1,0:T(8,128)} %get-tuple-element.94, f32[32,4096]{1,0:T(8,128)S(1)} %get-tuple-element.62, pred[]{:T(512)S(6)} %ne.47), kind=kLoop, calls=%fused_computation.155 | loop fusion | flops 786432 | bytes 2097153 | tf_op jit(solution)/shard_map/jit(_where)/select_n | solution.py:76
  146.6 20.8 %all-reduce = (f32[1]{0:T(128)}, f32[1]{0:T(128)}, f32[1]{0:T(128)}, f32[1]{0:T(128)}, f32[1]{0:T(128)}, /*index=5*/f32[1]{0:T(128)}) all-reduce(f32[1]{0:T(128)} %bitcast.8, f32[1]{0:T(128)} %bitcast.7, f32[1]{0:T(128)} %bitcast.6, f32[1]{0:T(128)} %bitcast.11, f32[1]{0:T(128)} %bitcast.10, ...), channel_id=1, replica_groups=mesh['blk'=8,'rows'=4] {'blk'}, use_global_device_ids=true, to_apply=%region_53.54 | all-reduce | flops 6 | bytes 48 | tf_op jit(solution)/shard_map/psum | solution.py:63
  167.4 4.3 %fusion.110 = f32[3]{0:T(128)} fusion(f32[1]{0:T(128)} %get-tuple-element.53, f32[1]{0:T(128)} %get-tuple-element.54, f32[1]{0:T(128)} %get-tuple-element.55, f32[1]{0:T(128)} %get-tuple-element.56, f32[1]{0:T(128)} %get-tuple-element.57, f32[1]{0:T(128)} %get-tuple-element.58), kind=kLoop, calls=%fused_computation.235 | loop fusion | flops 15 | bytes 36 | tf_op jit(solution)/shard_map/div | solution.py:83
  (209 shorter events, 42.0 us)
Async XLA Ops:
  0.6 1.2 copy-start
  2.8 1.4 collective-permute-start.21
  4.3 2.9 %copy-start.1 = (s32[3,16]{1,0:T(4,128)S(1)}, s32[3,16]{1,0:T(4,128)}, u32[]{:S(2)}) copy-start(s32[3,16]{1,0:T(4,128)} %param.24) | copy-start | bytes 580
  4.3 9.4 %collective-permute-start.22 = (f32[64,64]{1,0:T(8,128)S(1)}, f32[64,64]{1,0:T(8,128)S(1)}, u32[]{:S(2)}, u32[]{:S(2)}) collective-permute-start(f32[64,64]{1,0:T(8,128)S(1)} %add.39), channel_id=1, source_target_pairs={{0,2},{1,3},{2,0},{3,1},{4,6},{5,7},{6,4},{7,5},{8,10},{9,11},{10,... | collective-permute-start | bytes 49160 | tf_op jit(solution)/shard_map/ppermute | solution.py:56
  30.8 14.8 %collective-permute-start.5 = (f32[32,4096]{1,0:T(8,128)S(1)}, f32[32,4096]{1,0:T(8,128)}, u32[]{:S(2)}, u32[]{:S(2)}) collective-permute-start(f32[32,4096]{1,0:T(8,128)S(1)} %param.5), channel_id=1, source_target_pairs={{0,24},{4,28},{8,0},{12,4},{16,8},{20,12},{24,16},{28,20},{1,25},{... | collective-permute-start | bytes 1572872 | tf_op jit(solution)/shard_map/cond/branch_5_fun/ppermute | solution.py:16
  48.4 1.3 collective-permute-start.23
  49.7 6.6 %collective-permute-start.24 = (f32[64,64]{1,0:T(8,128)S(1)}, f32[64,64]{1,0:T(8,128)S(1)}, u32[]{:S(2)}, u32[]{:S(2)}) collective-permute-start(f32[64,64]{1,0:T(8,128)S(1)} %add.41), channel_id=1, source_target_pairs={{0,2},{1,3},{2,0},{3,1},{4,6},{5,7},{6,4},{7,5},{8,10},{9,11},{10,... | collective-permute-start | bytes 49160 | tf_op jit(solution)/shard_map/ppermute | solution.py:56
  74.6 26.9 %collective-permute-start.9 = (f32[32,4096]{1,0:T(8,128)S(1)}, f32[32,4096]{1,0:T(8,128)}, u32[]{:S(2)}, u32[]{:S(2)}) collective-permute-start(f32[32,4096]{1,0:T(8,128)S(1)} %param.9), channel_id=1, source_target_pairs={{0,12},{4,16},{8,20},{12,24},{16,28},{20,0},{24,4},{28,8},{1,13},{... | collective-permute-start | bytes 1572872 | tf_op jit(solution)/shard_map/cond/branch_2_fun/ppermute | solution.py:16
  104.2 1.3 collective-permute-start.25
  105.5 6.6 %collective-permute-start.26 = (f32[64,64]{1,0:T(8,128)S(1)}, f32[64,64]{1,0:T(8,128)S(1)}, u32[]{:S(2)}, u32[]{:S(2)}) collective-permute-start(f32[64,64]{1,0:T(8,128)S(1)} %add.43), channel_id=1, source_target_pairs={{0,2},{1,3},{2,0},{3,1},{4,6},{5,7},{6,4},{7,5},{8,10},{9,11},{10,... | collective-permute-start | bytes 49160 | tf_op jit(solution)/shard_map/ppermute | solution.py:56
  130.4 13.9 %collective-permute-start.20 = (f32[32,4096]{1,0:T(8,128)S(1)}, f32[32,4096]{1,0:T(8,128)}, u32[]{:S(2)}, u32[]{:S(2)}) collective-permute-start(f32[32,4096]{1,0:T(8,128)S(1)} %param.20), channel_id=1, source_target_pairs={{0,28},{4,0},{8,4},{12,8},{16,12},{20,16},{24,20},{28,24},{1,29},{... | collective-permute-start | bytes 1572872 | tf_op jit(solution)/shard_map/cond/branch_6_fun/ppermute | solution.py:16
